TPU v7x, 128 devices: a whole 4x4x4 slice. The times are simulated.
128 devices in a mesh: row: 16 (over y, x_lo, core), col: 8 (over x_hi, z).
Axes of the slice: x: 4 (x_hi: 2, x_lo: 2; x = x_hi * 2 + x_lo), y: 4, z: 4, core: 2. Of those that a mesh axis runs over, the one named last changes fastest.
Arguments:
- lower_inverse: float32 [16, 8, 1024, 1024], P('row', 'col'), may hold values from -1 to 2, as said below
- upper_inverse: float32 [16, 8, 1024, 1024], P('row', 'col'), may hold values from -1 to 2, as said below
- left_coupling: bfloat16 [16, 8, 512, 1024], P('row', 'col'), may hold values from -0.1875 to 0.1875
- right_pieces: float32 [8, 1024, 2048], P('col', None, 'row'), may hold values from -6 to 6
- interface_block: int32 [16, 8, 4], P('row', 'col'), may hold values from 0 to 7, all different within a row
- a_gg: float32 [16, 1024, 2048], P('row', 'col'), may hold values from -6 to 6
- panel_order: int32 [16], replicated, may hold values from 0 to 15, each once
Outputs:
- schur: float32 [16, 1024, 2048], P('row', 'col')
Inputs may be any that keep to these rules, and one draw needn't show every extreme that they name: `interface_block`: the 4 block ids of one subdomain are distinct. `panel_order`: A permutation of the column blocks. `lower_inverse`: lower triangular, diagonal between 1 and 2. `upper_inverse`: upper triangular, diagonal between 1 and 2.
All inputs are finite; a program needn't handle non-finite values.
Results may differ from a plain program's by a relative error of at most 0.0028.
Values sent between devices are 32-bit elements; how exact they have to be, the bound alone decides.
A program may use at most 128 MiB of HBM per device.

v0:
```python
import functools

import jax
import jax.numpy as jnp
from jax import lax
from jax.experimental import pallas as pl
from jax.experimental.pallas import tpu as pltpu
from jax.sharding import PartitionSpec as P

MESH = pl.DeviceIdType.MESH
F32, BF16 = jnp.float32, jnp.bfloat16

NI = 1024
WB = 128
CW = 2 * WB
NCH = 8
TB = 256

UP, DN = 48, 40
XU, XD = 16, 24
RA = UP + DN
XR = XU + XD
A_UP, A_DN, A_ALL = pl.ds(0, UP), pl.ds(UP, DN), pl.ds(0, RA)
X_UP, X_DN, X_ALL = pl.ds(RA, XU), pl.ds(RA + XU, XD), pl.ds(RA, XR)

CHUNKS = ((0, 0), (3, 0), (1, 0), (0, 1), (3, 1), (1, 1), (2, 0), (2, 1))


def coords():
    r, c = lax.axis_index("row"), lax.axis_index("col")
    return r // 4, (r // 2) % 2, r % 2, c // 4, c % 4


def device(y, xl, core, xh, z):
    return (y * 4 + xl * 2 + core, xh * 4 + z)


def split(x):
    hi = x.astype(BF16)
    return hi, (x - hi.astype(F32)).astype(BF16)


def main_kernel(
    ids, low_hbm, upp_hbm, left_hbm, piece_hbm, out,
    low32, upp32, left_v, panel, low_hi, low_lo, upp_hi, upp_lo, left_d,
    p_hi, p_lo, h_hi, h_lo, solved, part,
    rp2, rq2, fp, fq, fpa, fqa, fx2, rx, rxp2, rxq2, fxp, fxq, fxpa, fxqa,
    loc_sem, ag_s, ag_r, par_s, par_r, rs_s, rs_r,
):
    y, xl, core, xh, z = coords()
    partner = device(y, xl, 1 - core, xh, z)
    across = device(y, 1 - xl, core, xh, z)
    yp = device((y + 1) % 4, xl, core, xh, z)
    ym = device((y + 3) % 4, xl, core, xh, z)
    zp = device(y, xl, core, xh, (z + 1) % 4)
    zm = device(y, xl, core, xh, (z + 3) % 4)
    far = device(y, xl, core, 1 - xh, z)

    own = pltpu.make_async_copy(piece_hbm, panel.at[0, 0], loc_sem.at[0])
    own.start()
    loads = []
    for b in range(4):
        rows = pl.ds(b * TB, TB)
        cols = pl.ds(0, (b + 1) * TB)
        loads.append(pltpu.make_async_copy(low_hbm.at[rows, cols], low32.at[rows, cols], loc_sem.at[1 + b]))
    for b in range(4):
        rows = pl.ds(b * TB, TB)
        cols = pl.ds(b * TB, NI - b * TB)
        loads.append(pltpu.make_async_copy(upp_hbm.at[rows, cols], upp32.at[rows, cols], loc_sem.at[5 + b]))
    left_load = pltpu.make_async_copy(left_hbm, left_v, loc_sem.at[9])
    for copy in loads:
        copy.start()
    left_load.start()

    barrier = pltpu.get_barrier_semaphore()
    for peer in (partner, across, yp, ym, zp, zm, far):
        pl.semaphore_signal(barrier, inc=1, device_id=peer, device_id_type=MESH)
    pl.semaphore_wait(barrier, 7)

    def link(n, src, dst, peer):
        return pltpu.make_async_remote_copy(
            src_ref=panel.at[src, 0], dst_ref=panel.at[dst, 0], send_sem=ag_s.at[n],
            recv_sem=ag_r.at[dst], device_id=peer, device_id_type=MESH)

    links = (
        link(0, 0, 1, yp), link(1, 0, 2, ym), link(2, 0, 3, across),
        link(3, 3, 4, yp), link(4, 3, 5, ym), link(5, 1, 6, yp), link(6, 5, 7, ym))
    landing = {1: links[0], 2: links[1], 3: links[2], 4: links[3], 5: links[4], 6: links[5], 7: links[6]}

    def share(i):
        return pltpu.make_async_remote_copy(
            src_ref=panel.at[i, 0], dst_ref=panel.at[i, 1], send_sem=par_s.at[i],
            recv_sem=par_r.at[i], device_id=partner, device_id_type=MESH)

    own.wait()
    share(0).start()
    for n in (0, 1, 2):
        links[n].start()

    strip = 32
    for b in range(4):
        loads[b].wait()

        @pl.loop(0, TB // strip)
        def _(s, b=b):
            rows = pl.ds(pl.multiple_of(b * TB + s * strip, strip), strip)
            cols = pl.ds(0, (b + 1) * TB)
            low_hi[rows, cols], low_lo[rows, cols] = split(low32[rows, cols])
    for b in range(4):
        loads[4 + b].wait()

        @pl.loop(0, TB // strip)
        def _(s, b=b):
            rows = pl.ds(pl.multiple_of(b * TB + s * strip, strip), strip)
            cols = pl.ds(b * TB, NI - b * TB)
            upp_hi[rows, cols], upp_lo[rows, cols] = split(upp32[rows, cols])

    left_load.wait()
    for dx in range(2):
        for dz in range(4):
            block = ((xh + dx) % 2) * 4 + (z + dz) % 4
            place = jnp.int32(0)
            touched = jnp.int32(0)
            for k in range(4):
                hit = ids[k] == block
                place = jnp.where(hit, k, place)
                touched = jnp.where(hit, 1, touched)
            left_d[dx, dz] = jnp.where(touched > 0, left_v[place], jnp.zeros((WB, NI), BF16))

    def reduce_copies(i):
        def send(n, src, dst, peer):
            return pltpu.make_async_remote_copy(
                src_ref=src, dst_ref=dst.at[i], send_sem=rs_s.at[i, n], recv_sem=rs_r.at[i, n],
                device_id=peer, device_id_type=MESH)

        both = slice(None)
        return (
            send(0, part.at[i, both, 2, A_UP], rp2, zp),
            send(1, part.at[i, both, 2, A_DN], rq2, zm),
            send(2, part.at[i, both, 1, A_DN], fq, zp),
            send(3, part.at[i, both, 3, A_UP], fp, zm),
            send(4, part.at[i, 1, both, X_ALL], rx, far),
            send(5, part.at[i, both, 1, A_UP], fpa, zp),
            send(6, part.at[i, both, 3, A_DN], fqa, zm),
            send(7, part.at[i, 0, 2, X_UP], rxp2, zp),
            send(8, part.at[i, 0, 2, X_DN], rxq2, zm),
            send(9, part.at[i, 0, 1, X_DN], fxq, zp),
            send(10, part.at[i, 0, 3, X_UP], fxp, zm),
            send(11, part.at[i, 1, 0, A_ALL], fx2, far),
            send(12, part.at[i, 0, 1, X_UP], fxpa, zp),
            send(13, part.at[i, 0, 3, X_DN], fxqa, zm),
        )

    def multiply(i):
        for h in range(2):
            @pl.loop(0, 8)
            def _(s, h=h):
                rows = pl.ds(pl.multiple_of(s * WB, WB), WB)
                cols = pl.ds(h * WB, WB)
                p_hi[rows, cols], p_lo[rows, cols] = split(panel[i, h, rows, :])

        def dot(a, b):
            return jnp.dot(a, b, preferred_element_type=F32)

        for b in range(4):
            rows, cols = pl.ds(b * TB, TB), pl.ds(0, (b + 1) * TB)
            a_hi = low_hi[rows, cols]
            half = dot(a_hi, p_hi[cols]) + dot(a_hi, p_lo[cols]) + dot(low_lo[rows, cols], p_hi[cols])
            h_hi[rows, :], h_lo[rows, :] = split(half)
        for b in range(4):
            rows, cols = pl.ds(b * TB, TB), pl.ds(b * TB, NI - b * TB)
            a_hi = upp_hi[rows, cols]
            full = dot(a_hi, h_hi[cols]) + dot(a_hi, h_lo[cols]) + dot(upp_lo[rows, cols], h_hi[cols])
            solved[rows, :] = full.astype(BF16)
        for dx in range(2):
            for dz in range(4):
                part[i, dx, dz] = dot(left_d[dx, dz], solved[...])

    @pl.loop(0, NCH + 3)
    def _(step):
        for at, arrivals in ((1, (1, 3, 2)), (3, (4, 5)), (5, (6, 7))):
            @pl.when(step == at)
            def _(arrivals=arrivals):
                for a in arrivals:
                    landing[a].wait_recv()
                    for n in {1: (5,), 3: (3, 4), 5: (6,)}.get(a, ()):
                        links[n].start()
                    share(a).start()

        @pl.when(step < NCH)
        def _():
            share(step).wait_recv()
            multiply(step)
            copies = reduce_copies(step)
            for n in range(5):
                copies[n].start()

        @pl.when((step >= 1) & (step < NCH + 1))
        def _():
            i = step - 1
            copies = reduce_copies(i)
            copies[0].wait_recv()
            part[i, :, 1, A_UP] += rp2[i]
            copies[5].start()
            copies[1].wait_recv()
            part[i, :, 3, A_DN] += rq2[i]
            copies[6].start()
            copies[4].wait_recv()
            part[i, 0, :, X_ALL] += rx[i]
            for n in (7, 8, 9, 10):
                copies[n].start()

        @pl.when((step >= 2) & (step < NCH + 2))
        def _():
            i = step - 2
            copies = reduce_copies(i)
            for n in (2, 3, 5, 6):
                copies[n].wait_recv()
            part[i, :, 0, A_UP] += fp[i] + fpa[i]
            part[i, :, 0, A_DN] += fq[i] + fqa[i]
            copies[11].start()
            copies[7].wait_recv()
            part[i, 0, 1, X_UP] += rxp2[i]
            copies[12].start()
            copies[8].wait_recv()
            part[i, 0, 3, X_DN] += rxq2[i]
            copies[13].start()

        @pl.when(step >= 3)
        def _():
            i = step - 3
            copies = reduce_copies(i)
            for n in (9, 10, 11, 12, 13):
                copies[n].wait_recv()
            out[i, A_ALL] = part[i, 0, 0, A_ALL] + fx2[i]
            out[i, X_UP] = part[i, 0, 0, X_UP] + (fxp[i] + fxpa[i])
            out[i, X_DN] = part[i, 0, 0, X_DN] + (fxq[i] + fxqa[i])

    for copy in links:
        copy.wait_send()

    @pl.loop(0, NCH)
    def _(i):
        share(i).wait_send()
        for copy in reduce_copies(i):
            copy.wait_send()


def place_kernel(order, owned, base, out):
    y, xl, core, _, _ = coords()
    for j, (dy, dx) in enumerate(CHUNKS):
        for h in range(2):
            source = ((y + dy) % 4) * 4 + ((xl + dx) % 2) * 2 + (core + h) % 2
            cols = pl.ds(pl.multiple_of(order[source] * WB, WB), WB)
            out[:, cols] = base[:, cols] - owned[j, :, h * WB:(h + 1) * WB]


def per_device(lower_inverse, upper_inverse, left_coupling, right_pieces, interface_block, a_gg, panel_order):
    vmem = pl.BlockSpec(memory_space=pltpu.VMEM)
    smem = pl.BlockSpec(memory_space=pltpu.SMEM)
    hbm = pl.BlockSpec(memory_space=pltpu.HBM)

    def buf(*shape, dtype=F32):
        return pltpu.VMEM(shape, dtype)

    dma = pltpu.SemaphoreType.DMA
    owned = pl.pallas_call(
        main_kernel,
        name="assemble",
        out_shape=jax.ShapeDtypeStruct((NCH, WB, CW), F32),
        in_specs=[smem, hbm, hbm, hbm, hbm],
        out_specs=vmem,
        scratch_shapes=[
            buf(NI, NI), buf(NI, NI), buf(4, WB, NI, dtype=BF16), buf(NCH, 2, NI, WB),
            buf(NI, NI, dtype=BF16), buf(NI, NI, dtype=BF16), buf(NI, NI, dtype=BF16), buf(NI, NI, dtype=BF16),
            buf(2, 4, WB, NI, dtype=BF16),
            buf(NI, CW, dtype=BF16), buf(NI, CW, dtype=BF16), buf(NI, CW, dtype=BF16), buf(NI, CW, dtype=BF16),
            buf(NI, CW, dtype=BF16), buf(NCH, 2, 4, WB, CW),
            buf(NCH, 2, UP, CW), buf(NCH, 2, DN, CW), buf(NCH, 2, UP, CW), buf(NCH, 2, DN, CW),
            buf(NCH, 2, UP, CW), buf(NCH, 2, DN, CW), buf(NCH, RA, CW),
            buf(NCH, 4, XR, CW), buf(NCH, XU, CW), buf(NCH, XD, CW), buf(NCH, XU, CW), buf(NCH, XD, CW),
            buf(NCH, XU, CW), buf(NCH, XD, CW),
            dma((10,)), dma((7,)), dma((NCH,)), dma((NCH,)), dma((NCH,)), dma((NCH, 14)), dma((NCH, 14)),
        ],
        compiler_params=pltpu.CompilerParams(
            collective_id=0, has_side_effects=True, vmem_limit_bytes=60 * 2**20),
    )(
        interface_block[0, 0], lower_inverse[0, 0], upper_inverse[0, 0],
        left_coupling[0, 0].reshape(4, WB, NI), right_pieces[0])
    schur = pl.pallas_call(
        place_kernel,
        name="place",
        out_shape=jax.ShapeDtypeStruct(a_gg.shape[1:], F32),
        in_specs=[smem, vmem, vmem],
        out_specs=vmem,
    )(panel_order, owned, a_gg[0])
    return schur[None]


def solution(mesh):
    return jax.shard_map(
        per_device,
        mesh=mesh,
        in_specs=(
            P("row", "col", None, None),
            P("row", "col", None, None),
            P("row", "col", None, None),
            P("col", None, "row"),
            P("row", "col", None),
            P("row", "col", None),
            P(),
        ),
        out_specs=P("row", "col", None),
        check_vma=False,
    )
```

profile of v0, /device:TPU:0, one launch (start us, length us, event | category | flops | bytes accessed | tf_op | source)
XLA Modules:
  0.0 97.3 jit_solution(14128460501394137869)
XLA Ops:
  0.0 94.5 %assemble.1.owned = f32[8,128,256]{2,1,0:T(8,128)} custom-call(s32[4]{0:T(128)} %bitcast.12, f32[1024,1024]{1,0:T(8,128)} %bitcast.7, f32[1024,1024]{1,0:T(8,128)} %bitcast.8, bf16[4,128,1024]{2,1,0:T(8,128)(2,1)} %bitcast.10, f32[1024,128]{1,0:T(8,128)} %bitcast.11), custom_call_target="tpu_custom_call" | custom-call | tf_op jit(solution)/shard_map/assemble/pallas_call | solution.py:267
  94.5 2.8 %place.1 = f32[128,2048]{1,0:T(8,128)} custom-call(s32[16]{0:T(128)} %order.1, f32[8,128,256]{2,1,0:T(8,128)} %assemble.1.owned, f32[128,2048]{1,0:T(8,128)} %bitcast.9), custom_call_target="tpu_custom_call" | custom-call | tf_op jit(solution)/shard_map/place/pallas_call | solution.py:290
where the time goes:
time: 97.4 us; the launch traced here: 97.3 us
  Pallas kernels  97.3 us (100%)
    pallas_call x1, Pallas kernels, per_device(): pl.pallas_call(main_kernel, name='assemble', out_shape=jax.ShapeDtypeStru...  94.5 us
    pallas_call x1, Pallas kernels, per_device(): pl.pallas_call(place_kernel, name='place', out_shape=jax.ShapeDtypeStruct...  2.76 us

commit v1 on v0

--- a/solution.py
+++ b/solution.py
@@ -23,7 +23,7 @@
 A_UP, A_DN, A_ALL = pl.ds(0, UP), pl.ds(UP, DN), pl.ds(0, RA)
 X_UP, X_DN, X_ALL = pl.ds(RA, XU), pl.ds(RA + XU, XD), pl.ds(RA, XR)
 
-CHUNKS = ((0, 0), (3, 0), (1, 0), (0, 1), (3, 1), (1, 1), (2, 0), (2, 1))
+CHUNKS = ((0, 0), (-1, 0), (1, 0), (0, 1), (2, 0), (-1, 1), (1, 1), (2, 1))
 
 
 def coords():
@@ -44,14 +44,14 @@
     ids, low_hbm, upp_hbm, left_hbm, piece_hbm, out,
     low32, upp32, left_v, panel, low_hi, low_lo, upp_hi, upp_lo, left_d,
     p_hi, p_lo, h_hi, h_lo, solved, part,
-    rp2, rq2, fp, fq, fpa, fqa, fx2, rx, rxp2, rxq2, fxp, fxq, fxpa, fxqa,
+    rp2, rq2, rx, fa1, fa3, rxp2, rxq2, fx2, fx1, fx3,
     loc_sem, ag_s, ag_r, par_s, par_r, rs_s, rs_r,
 ):
     y, xl, core, xh, z = coords()
     partner = device(y, xl, 1 - core, xh, z)
     across = device(y, 1 - xl, core, xh, z)
-    yp = device((y + 1) % 4, xl, core, xh, z)
-    ym = device((y + 3) % 4, xl, core, xh, z)
+    ahead = device((y + 1 + 2 * core) % 4, xl, core, xh, z)
+    behind = device((y + 3 + 2 * core) % 4, xl, core, xh, z)
     zp = device(y, xl, core, xh, (z + 1) % 4)
     zm = device(y, xl, core, xh, (z + 3) % 4)
     far = device(y, xl, core, 1 - xh, z)
@@ -73,7 +73,7 @@
     left_load.start()
 
     barrier = pltpu.get_barrier_semaphore()
-    for peer in (partner, across, yp, ym, zp, zm, far):
+    for peer in (partner, across, ahead, behind, zp, zm, far):
         pl.semaphore_signal(barrier, inc=1, device_id=peer, device_id_type=MESH)
     pl.semaphore_wait(barrier, 7)
 
@@ -82,10 +82,9 @@
             src_ref=panel.at[src, 0], dst_ref=panel.at[dst, 0], send_sem=ag_s.at[n],
             recv_sem=ag_r.at[dst], device_id=peer, device_id_type=MESH)
 
-    links = (
-        link(0, 0, 1, yp), link(1, 0, 2, ym), link(2, 0, 3, across),
-        link(3, 3, 4, yp), link(4, 3, 5, ym), link(5, 1, 6, yp), link(6, 5, 7, ym))
-    landing = {1: links[0], 2: links[1], 3: links[2], 4: links[3], 5: links[4], 6: links[5], 7: links[6]}
+    links = {
+        1: link(0, 0, 1, ahead), 2: link(1, 0, 2, behind), 3: link(2, 0, 3, across), 4: link(3, 1, 4, ahead),
+        5: link(4, 3, 5, ahead), 6: link(5, 3, 6, behind), 7: link(6, 6, 7, behind)}
 
     def share(i):
         return pltpu.make_async_remote_copy(
@@ -94,8 +93,8 @@
 
     own.wait()
     share(0).start()
-    for n in (0, 1, 2):
-        links[n].start()
+    links[1].start()
+    links[3].start()
 
     strip = 32
     for b in range(4):
@@ -134,22 +133,28 @@
                 device_id=peer, device_id_type=MESH)
 
         both = slice(None)
-        return (
-            send(0, part.at[i, both, 2, A_UP], rp2, zp),
-            send(1, part.at[i, both, 2, A_DN], rq2, zm),
-            send(2, part.at[i, both, 1, A_DN], fq, zp),
-            send(3, part.at[i, both, 3, A_UP], fp, zm),
-            send(4, part.at[i, 1, both, X_ALL], rx, far),
-            send(5, part.at[i, both, 1, A_UP], fpa, zp),
-            send(6, part.at[i, both, 3, A_DN], fqa, zm),
-            send(7, part.at[i, 0, 2, X_UP], rxp2, zp),
-            send(8, part.at[i, 0, 2, X_DN], rxq2, zm),
-            send(9, part.at[i, 0, 1, X_DN], fxq, zp),
-            send(10, part.at[i, 0, 3, X_UP], fxp, zm),
-            send(11, part.at[i, 1, 0, A_ALL], fx2, far),
-            send(12, part.at[i, 0, 1, X_UP], fxpa, zp),
-            send(13, part.at[i, 0, 3, X_DN], fxqa, zm),
-        )
+        return {
+            0: lambda: send(0, part.at[i, both, 2, A_UP], rp2, zp),
+            1: lambda: send(1, part.at[i, both, 2, A_DN], rq2, zm),
+            2: lambda: send(2, part.at[i, 1, both, X_ALL], rx, far),
+            3: lambda: send(3, part.at[i, both, 1, A_ALL], fa1, zp),
+            4: lambda: send(4, part.at[i, both, 3, A_ALL], fa3, zm),
+            5: lambda: send(5, part.at[i, 0, 2, X_UP], rxp2, zp),
+            6: lambda: send(6, part.at[i, 0, 2, X_DN], rxq2, zm),
+            7: lambda: send(7, part.at[i, 1, 0, A_ALL], fx2, far),
+            8: lambda: send(8, part.at[i, 0, 1, X_ALL], fx1, zp),
+            9: lambda: send(9, part.at[i, 0, 3, X_ALL], fx3, zm),
+        }
+
+    def start(i, *which):
+        copies = reduce_copies(i)
+        for n in which:
+            copies[n]().start()
+
+    def arrive(i, *which):
+        copies = reduce_copies(i)
+        for n in which:
+            copies[n]().wait_recv()
 
     def multiply(i):
         for h in range(2):
@@ -176,81 +181,111 @@
             for dz in range(4):
                 part[i, dx, dz] = dot(left_d[dx, dz], solved[...])
 
-    @pl.loop(0, NCH + 3)
+    def first(i):
+        arrive(i, 0)
+        part[i, :, 1, A_UP] += rp2[i]
+        start(i, 3)
+        arrive(i, 1)
+        part[i, :, 3, A_DN] += rq2[i]
+        start(i, 4)
+
+    def second(i):
+        arrive(i, 3, 4)
+        part[i, :, 0, A_ALL] += fa1[i] + fa3[i]
+        start(i, 7)
+
+    def cross(i):
+        arrive(i, 2)
+        part[i, 0, :, X_ALL] += rx[i]
+        start(i, 5, 6)
+
+    def along(i):
+        arrive(i, 5)
+        part[i, 0, 1, X_UP] += rxp2[i]
+        start(i, 8)
+        arrive(i, 6)
+        part[i, 0, 3, X_DN] += rxq2[i]
+        start(i, 9)
+
+    def finish(i):
+        arrive(i, 7)
+        out[i, A_ALL] = part[i, 0, 0, A_ALL] + fx2[i]
+        arrive(i, 8, 9)
+        out[i, X_ALL] = part[i, 0, 0, X_ALL] + (fx1[i] + fx3[i])
+
+    def pass_on(a, *then):
+        links[a].wait_recv()
+        share(a).start()
+        for n in then:
+            links[n].start()
+
+    @pl.loop(0, NCH)
     def _(step):
-        for at, arrivals in ((1, (1, 3, 2)), (3, (4, 5)), (5, (6, 7))):
-            @pl.when(step == at)
-            def _(arrivals=arrivals):
-                for a in arrivals:
-                    landing[a].wait_recv()
-                    for n in {1: (5,), 3: (3, 4), 5: (6,)}.get(a, ()):
-                        links[n].start()
-                    share(a).start()
-
-        @pl.when(step < NCH)
-        def _():
-            share(step).wait_recv()
-            multiply(step)
-            copies = reduce_copies(step)
-            for n in range(5):
-                copies[n].start()
-
-        @pl.when((step >= 1) & (step < NCH + 1))
-        def _():
-            i = step - 1
-            copies = reduce_copies(i)
-            copies[0].wait_recv()
-            part[i, :, 1, A_UP] += rp2[i]
-            copies[5].start()
-            copies[1].wait_recv()
-            part[i, :, 3, A_DN] += rq2[i]
-            copies[6].start()
-            copies[4].wait_recv()
-            part[i, 0, :, X_ALL] += rx[i]
-            for n in (7, 8, 9, 10):
-                copies[n].start()
-
-        @pl.when((step >= 2) & (step < NCH + 2))
-        def _():
-            i = step - 2
-            copies = reduce_copies(i)
-            for n in (2, 3, 5, 6):
-                copies[n].wait_recv()
-            part[i, :, 0, A_UP] += fp[i] + fpa[i]
-            part[i, :, 0, A_DN] += fq[i] + fqa[i]
-            copies[11].start()
-            copies[7].wait_recv()
-            part[i, 0, 1, X_UP] += rxp2[i]
-            copies[12].start()
-            copies[8].wait_recv()
-            part[i, 0, 3, X_DN] += rxq2[i]
-            copies[13].start()
-
-        @pl.when(step >= 3)
-        def _():
-            i = step - 3
-            copies = reduce_copies(i)
-            for n in (9, 10, 11, 12, 13):
-                copies[n].wait_recv()
-            out[i, A_ALL] = part[i, 0, 0, A_ALL] + fx2[i]
-            out[i, X_UP] = part[i, 0, 0, X_UP] + (fxp[i] + fxpa[i])
-            out[i, X_DN] = part[i, 0, 0, X_DN] + (fxq[i] + fxqa[i])
-
-    for copy in links:
-        copy.wait_send()
+        @pl.when(step == 1)
+        def _():
+            pass_on(1)
+            first(0)
+
+        @pl.when(step == 2)
+        def _():
+            pass_on(2, 4)
+            pass_on(3, 5, 6)
+            first(1)
+
+        @pl.when(step == 4)
+        def _():
+            first(3)
+            pass_on(4)
+            pass_on(5)
+
+        @pl.when(step == 5)
+        def _():
+            pass_on(6, 7)
+
+        @pl.when(step == 7)
+        def _():
+            pass_on(7)
+
+        share(step).wait_recv()
+        multiply(step)
+        start(step, 0, 1, 2)
+
+        @pl.when(step == 0)
+        def _():
+            links[1].wait_send()
+            links[2].start()
+
+        @pl.when((step == 3) | (step >= 5))
+        def _():
+            first(step - 1)
+
+        for lag, stage in ((2, cross), (2, second), (3, along), (5, finish)):
+            @pl.when(step >= lag)
+            def _(lag=lag, stage=stage):
+                stage(step - lag)
+
+    for i, stage in (
+        (6, cross), (7, first), (7, cross), (6, second), (5, along), (6, along), (7, second), (7, along),
+        (3, finish), (4, finish), (5, finish), (6, finish), (7, finish),
+    ):
+        stage(i)
+
+    for n in range(2, 8):
+        links[n].wait_send()
 
     @pl.loop(0, NCH)
     def _(i):
         share(i).wait_send()
-        for copy in reduce_copies(i):
-            copy.wait_send()
+        for copy in reduce_copies(i).values():
+            copy().wait_send()
 
 
 def place_kernel(order, owned, base, out):
     y, xl, core, _, _ = coords()
     for j, (dy, dx) in enumerate(CHUNKS):
         for h in range(2):
-            source = ((y + dy) % 4) * 4 + ((xl + dx) % 2) * 2 + (core + h) % 2
+            holder = (core + h) % 2
+            source = ((y + 4 + dy * (1 - 2 * holder)) % 4) * 4 + ((xl + dx) % 2) * 2 + holder
             cols = pl.ds(pl.multiple_of(order[source] * WB, WB), WB)
             out[:, cols] = base[:, cols] - owned[j, :, h * WB:(h + 1) * WB]
 
@@ -276,11 +311,9 @@
             buf(2, 4, WB, NI, dtype=BF16),
             buf(NI, CW, dtype=BF16), buf(NI, CW, dtype=BF16), buf(NI, CW, dtype=BF16), buf(NI, CW, dtype=BF16),
             buf(NI, CW, dtype=BF16), buf(NCH, 2, 4, WB, CW),
-            buf(NCH, 2, UP, CW), buf(NCH, 2, DN, CW), buf(NCH, 2, UP, CW), buf(NCH, 2, DN, CW),
-            buf(NCH, 2, UP, CW), buf(NCH, 2, DN, CW), buf(NCH, RA, CW),
-            buf(NCH, 4, XR, CW), buf(NCH, XU, CW), buf(NCH, XD, CW), buf(NCH, XU, CW), buf(NCH, XD, CW),
-            buf(NCH, XU, CW), buf(NCH, XD, CW),
-            dma((10,)), dma((7,)), dma((NCH,)), dma((NCH,)), dma((NCH,)), dma((NCH, 14)), dma((NCH, 14)),
+            buf(NCH, 2, UP, CW), buf(NCH, 2, DN, CW), buf(NCH, 4, XR, CW), buf(NCH, 2, RA, CW), buf(NCH, 2, RA, CW),
+            buf(NCH, XU, CW), buf(NCH, XD, CW), buf(NCH, RA, CW), buf(NCH, XR, CW), buf(NCH, XR, CW),
+            dma((10,)), dma((7,)), dma((NCH,)), dma((NCH,)), dma((NCH,)), dma((NCH, 10)), dma((NCH, 10)),
         ],
         compiler_params=pltpu.CompilerParams(
             collective_id=0, has_side_effects=True, vmem_limit_bytes=60 * 2**20),

time: 97.4 us -> 87 us (0.89); the launches traced: 97.3 us -> 85.6 us
  Pallas kernels: 97.3 us -> 85.6 us
    pallas_call x1, Pallas kernels: 94.5 us -> 82.8 us  [per_device(): pl.pallas_call(main_kernel, name='assemble', out_shape=jax.ShapeDtypeStru...]
where the time goes in v1:
time: 87 us; the launch traced here: 85.6 us
  Pallas kernels  85.6 us (98%)
    pallas_call x1, Pallas kernels, per_device(): pl.pallas_call(main_kernel, name='assemble', out_shape=jax.ShapeDtypeStru...  82.8 us
    pallas_call x1, Pallas kernels, per_device(): pl.pallas_call(place_kernel, name='place', out_shape=jax.ShapeDtypeStruct...  2.76 us

profile of v1, /device:TPU:0, one launch (start us, length us, event | category | flops | bytes accessed | tf_op | source)
XLA Modules:
  0.0 85.6 jit_solution(13556411850580336241)
XLA Ops:
  0.0 82.8 %assemble.1.owned = f32[8,128,256]{2,1,0:T(8,128)} custom-call(s32[4]{0:T(128)} %bitcast.12, f32[1024,1024]{1,0:T(8,128)} %bitcast.7, f32[1024,1024]{1,0:T(8,128)} %bitcast.8, bf16[4,128,1024]{2,1,0:T(8,128)(2,1)} %bitcast.10, f32[1024,128]{1,0:T(8,128)} %bitcast.11), custom_call_target="tpu_custom_call" | custom-call | tf_op jit(solution)/shard_map/assemble/pallas_call | solution.py:302
  82.8 2.8 %place.1 = f32[128,2048]{1,0:T(8,128)} custom-call(s32[16]{0:T(128)} %order.1, f32[8,128,256]{2,1,0:T(8,128)} %assemble.1.owned, f32[128,2048]{1,0:T(8,128)} %bitcast.9), custom_call_target="tpu_custom_call" | custom-call | tf_op jit(solution)/shard_map/place/pallas_call | solution.py:323

commit v2 on v1

--- a/solution.py
+++ b/solution.py
@@ -16,8 +16,8 @@
 NCH = 8
 TB = 256
 
-UP, DN = 48, 40
-XU, XD = 16, 24
+UP, DN = 40, 32
+XU, XD = 24, 32
 RA = UP + DN
 XR = XU + XD
 A_UP, A_DN, A_ALL = pl.ds(0, UP), pl.ds(UP, DN), pl.ds(0, RA)
@@ -41,10 +41,10 @@
 
 
 def main_kernel(
-    ids, low_hbm, upp_hbm, left_hbm, piece_hbm, out,
+    ids, order, low_hbm, upp_hbm, left_hbm, piece_hbm, base_hbm, out,
     low32, upp32, left_v, panel, low_hi, low_lo, upp_hi, upp_lo, left_d,
     p_hi, p_lo, h_hi, h_lo, solved, part,
-    rp2, rq2, rx, fa1, fa3, rxp2, rxq2, fx2, fx1, fx3,
+    rp2, rq2, rx, fa1, fa3, rxp2, rxq2, fx2, fx1, fx3, base, total, origin,
     loc_sem, ag_s, ag_r, par_s, par_r, rs_s, rs_r,
 ):
     y, xl, core, xh, z = coords()
@@ -71,6 +71,8 @@
     for copy in loads:
         copy.start()
     left_load.start()
+    base_load = pltpu.make_async_copy(base_hbm, base, loc_sem.at[10])
+    base_load.start()
 
     barrier = pltpu.get_barrier_semaphore()
     for peer in (partner, across, ahead, behind, zp, zm, far):
@@ -209,9 +211,13 @@
 
     def finish(i):
         arrive(i, 7)
-        out[i, A_ALL] = part[i, 0, 0, A_ALL] + fx2[i]
+        rows = part[i, 0, 0, A_ALL] + fx2[i]
+        for h in range(2):
+            total[2 * i + h, A_ALL] = rows[:, h * WB:(h + 1) * WB]
         arrive(i, 8, 9)
-        out[i, X_ALL] = part[i, 0, 0, X_ALL] + (fx1[i] + fx3[i])
+        rows = part[i, 0, 0, X_ALL] + (fx1[i] + fx3[i])
+        for h in range(2):
+            total[2 * i + h, X_ALL] = rows[:, h * WB:(h + 1) * WB]
 
     def pass_on(a, *then):
         links[a].wait_recv()
@@ -264,12 +270,28 @@
             def _(lag=lag, stage=stage):
                 stage(step - lag)
 
+    base_load.wait()
+    places = []
+    for dy, dx in CHUNKS:
+        for h in range(2):
+            holder = (core + h) % 2
+            places.append(order[((y + 4 + dy * (1 - 2 * holder)) % 4) * 4 + ((xl + dx) % 2) * 2 + holder])
+    for p in range(2 * NCH):
+        found = jnp.int32(0)
+        for t in range(2 * NCH):
+            found = jnp.where(places[t] == p, t, found)
+        origin[p] = found
+
     for i, stage in (
         (6, cross), (7, first), (7, cross), (6, second), (5, along), (6, along), (7, second), (7, along),
         (3, finish), (4, finish), (5, finish), (6, finish), (7, finish),
     ):
         stage(i)
 
+    for p in range(2 * NCH):
+        cols = slice(p * WB, (p + 1) * WB)
+        out[:, cols] = base[:, cols] - total[origin[p]]
+
     for n in range(2, 8):
         links[n].wait_send()
 
@@ -280,16 +302,6 @@
             copy().wait_send()
 
 
-def place_kernel(order, owned, base, out):
-    y, xl, core, _, _ = coords()
-    for j, (dy, dx) in enumerate(CHUNKS):
-        for h in range(2):
-            holder = (core + h) % 2
-            source = ((y + 4 + dy * (1 - 2 * holder)) % 4) * 4 + ((xl + dx) % 2) * 2 + holder
-            cols = pl.ds(pl.multiple_of(order[source] * WB, WB), WB)
-            out[:, cols] = base[:, cols] - owned[j, :, h * WB:(h + 1) * WB]
-
-
 def per_device(lower_inverse, upper_inverse, left_coupling, right_pieces, interface_block, a_gg, panel_order):
     vmem = pl.BlockSpec(memory_space=pltpu.VMEM)
     smem = pl.BlockSpec(memory_space=pltpu.SMEM)
@@ -298,12 +310,15 @@
     def buf(*shape, dtype=F32):
         return pltpu.VMEM(shape, dtype)
 
+    def fixed(x):
+        return pltpu.with_memory_space_constraint(x, pltpu.HBM)
+
     dma = pltpu.SemaphoreType.DMA
-    owned = pl.pallas_call(
+    schur = pl.pallas_call(
         main_kernel,
         name="assemble",
-        out_shape=jax.ShapeDtypeStruct((NCH, WB, CW), F32),
-        in_specs=[smem, hbm, hbm, hbm, hbm],
+        out_shape=jax.ShapeDtypeStruct(a_gg.shape[1:], F32),
+        in_specs=[smem, smem, hbm, hbm, hbm, hbm, hbm],
         out_specs=vmem,
         scratch_shapes=[
             buf(NI, NI), buf(NI, NI), buf(4, WB, NI, dtype=BF16), buf(NCH, 2, NI, WB),
@@ -313,20 +328,14 @@
             buf(NI, CW, dtype=BF16), buf(NCH, 2, 4, WB, CW),
             buf(NCH, 2, UP, CW), buf(NCH, 2, DN, CW), buf(NCH, 4, XR, CW), buf(NCH, 2, RA, CW), buf(NCH, 2, RA, CW),
             buf(NCH, XU, CW), buf(NCH, XD, CW), buf(NCH, RA, CW), buf(NCH, XR, CW), buf(NCH, XR, CW),
-            dma((10,)), dma((7,)), dma((NCH,)), dma((NCH,)), dma((NCH,)), dma((NCH, 10)), dma((NCH, 10)),
+            buf(WB, a_gg.shape[2]), buf(2 * NCH, WB, WB), pltpu.SMEM((2 * NCH,), jnp.int32),
+            dma((11,)), dma((7,)), dma((NCH,)), dma((NCH,)), dma((NCH,)), dma((NCH, 10)), dma((NCH, 10)),
         ],
         compiler_params=pltpu.CompilerParams(
-            collective_id=0, has_side_effects=True, vmem_limit_bytes=60 * 2**20),
+            collective_id=0, has_side_effects=True, vmem_limit_bytes=52 * 2**20),
     )(
-        interface_block[0, 0], lower_inverse[0, 0], upper_inverse[0, 0],
-        left_coupling[0, 0].reshape(4, WB, NI), right_pieces[0])
-    schur = pl.pallas_call(
-        place_kernel,
-        name="place",
-        out_shape=jax.ShapeDtypeStruct(a_gg.shape[1:], F32),
-        in_specs=[smem, vmem, vmem],
-        out_specs=vmem,
-    )(panel_order, owned, a_gg[0])
+        fixed(interface_block[0, 0]), fixed(panel_order), fixed(lower_inverse[0, 0]), fixed(upper_inverse[0, 0]),
+        fixed(left_coupling[0, 0].reshape(4, WB, NI)), fixed(right_pieces[0]), fixed(a_gg[0]))
     return schur[None]
 
 

time: 87 us -> 81.7 us (0.939)
  Pallas kernels: 85.6 us -> 79.9 us
  local copies, waits for them, and re-layouts: 0 us -> 0.97 us
    pallas_call x1, Pallas kernels: 82.8 us -> 79.9 us  [per_device(): pl.pallas_call(main_kernel, name='assemble', out_shape=jax.ShapeDtypeStru...]
    pallas_call x1 -> x0, Pallas kernels: 2.76 us -> none  [per_device(): pl.pallas_call(place_kernel, name='place', out_shape=jax.ShapeDtypeStruct...]
    unnamed x0 -> x1, local copies, waits for them, and re-layouts: none -> 0.97 us
where the time goes in v2:
time: 81.7 us; the launch traced here: 80.8 us
  Pallas kernels  79.9 us (98%)
  local copies, waits for them, and re-layouts  0.97 us (1%)
    pallas_call x1, Pallas kernels, per_device(): pl.pallas_call(main_kernel, name='assemble', out_shape=jax.ShapeDtypeStru...  79.9 us

profile of v2, /device:TPU:0, one launch (start us, length us, event | category | flops | bytes accessed | tf_op | source)
XLA Modules:
  0.0 80.8 jit_solution(3195114220097507752)
XLA Ops:
  0.0 79.9 %assemble.1 = f32[128,2048]{1,0:T(8,128)S(1)} custom-call(s32[4]{0:T(128)} %bitcast.13, s32[16]{0:T(128)} %order.1, f32[1024,1024]{1,0:T(8,128)} %bitcast.8, f32[1024,1024]{1,0:T(8,128)} %bitcast.9, bf16[4,128,1024]{2,1,0:T(8,128)(2,1)} %bitcast.10, f32[1024,128]{1,0:T(8,128)} %bitcast.12, f32[128,2048]{1,0:T(8,128)} %bitcast.11), custom_call_target="tpu_custom_call" | custom-call | tf_op jit(solution)/shard_map/assemble/pallas_call | solution.py:317
  79.9 1.0 %copy.9 = f32[1,128,2048]{2,1,0:T(8,128)} copy(f32[1,128,2048]{2,1,0:T(8,128)S(1)} %bitcast.7) | data formatting | bytes 2097152

commit v3 on v2

--- a/solution.py
+++ b/solution.py
@@ -88,10 +88,10 @@
         1: link(0, 0, 1, ahead), 2: link(1, 0, 2, behind), 3: link(2, 0, 3, across), 4: link(3, 1, 4, ahead),
         5: link(4, 3, 5, ahead), 6: link(5, 3, 6, behind), 7: link(6, 6, 7, behind)}
 
-    def share(i):
+    def share(i, at=None):
         return pltpu.make_async_remote_copy(
-            src_ref=panel.at[i, 0], dst_ref=panel.at[i, 1], send_sem=par_s.at[i],
-            recv_sem=par_r.at[i], device_id=partner, device_id_type=MESH)
+            src_ref=panel.at[i, 0], dst_ref=panel.at[i, 1], send_sem=par_s,
+            recv_sem=par_r.at[i if at is None else at], device_id=partner, device_id_type=MESH)
 
     own.wait()
     share(0).start()
@@ -126,12 +126,14 @@
                 hit = ids[k] == block
                 place = jnp.where(hit, k, place)
                 touched = jnp.where(hit, 1, touched)
-            left_d[dx, dz] = jnp.where(touched > 0, left_v[place], jnp.zeros((WB, NI), BF16))
-
-    def reduce_copies(i):
+            left_d[dx, dz * WB:(dz + 1) * WB] = jnp.where(touched > 0, left_v[place], jnp.zeros((WB, NI), BF16))
+
+    def reduce_copies(i, at=None):
+        at = i if at is None else at
+
         def send(n, src, dst, peer):
             return pltpu.make_async_remote_copy(
-                src_ref=src, dst_ref=dst.at[i], send_sem=rs_s.at[i, n], recv_sem=rs_r.at[i, n],
+                src_ref=src, dst_ref=dst.at[i], send_sem=rs_s.at[n], recv_sem=rs_r.at[at, n],
                 device_id=peer, device_id_type=MESH)
 
         both = slice(None)
@@ -139,8 +141,10 @@
             0: lambda: send(0, part.at[i, both, 2, A_UP], rp2, zp),
             1: lambda: send(1, part.at[i, both, 2, A_DN], rq2, zm),
             2: lambda: send(2, part.at[i, 1, both, X_ALL], rx, far),
-            3: lambda: send(3, part.at[i, both, 1, A_ALL], fa1, zp),
-            4: lambda: send(4, part.at[i, both, 3, A_ALL], fa3, zm),
+            3: lambda: send(3, part.at[i, 1, 1, A_ALL], fa1.at[1], zp),
+            4: lambda: send(4, part.at[i, 1, 3, A_ALL], fa3.at[1], zm),
+            10: lambda: send(10, part.at[i, 0, 1, A_ALL], fa1.at[0], zp),
+            11: lambda: send(11, part.at[i, 0, 3, A_ALL], fa3.at[0], zm),
             5: lambda: send(5, part.at[i, 0, 2, X_UP], rxp2, zp),
             6: lambda: send(6, part.at[i, 0, 2, X_DN], rxq2, zm),
             7: lambda: send(7, part.at[i, 1, 0, A_ALL], fx2, far),
@@ -172,28 +176,29 @@
         for b in range(4):
             rows, cols = pl.ds(b * TB, TB), pl.ds(0, (b + 1) * TB)
             a_hi = low_hi[rows, cols]
-            half = dot(a_hi, p_hi[cols]) + dot(a_hi, p_lo[cols]) + dot(low_lo[rows, cols], p_hi[cols])
+            both = dot(jnp.concatenate([a_hi, low_lo[rows, cols]], axis=0), p_hi[cols])
+            half = both[:TB] + both[TB:] + dot(a_hi, p_lo[cols])
             h_hi[rows, :], h_lo[rows, :] = split(half)
         for b in range(4):
             rows, cols = pl.ds(b * TB, TB), pl.ds(b * TB, NI - b * TB)
             a_hi = upp_hi[rows, cols]
-            full = dot(a_hi, h_hi[cols]) + dot(a_hi, h_lo[cols]) + dot(upp_lo[rows, cols], h_hi[cols])
+            both = dot(jnp.concatenate([a_hi, upp_lo[rows, cols]], axis=0), h_hi[cols])
+            full = both[:TB] + both[TB:] + dot(a_hi, h_lo[cols])
             solved[rows, :] = full.astype(BF16)
         for dx in range(2):
-            for dz in range(4):
-                part[i, dx, dz] = dot(left_d[dx, dz], solved[...])
+            part[i, dx] = dot(left_d[dx], solved[...]).reshape(4, WB, CW)
 
     def first(i):
         arrive(i, 0)
         part[i, :, 1, A_UP] += rp2[i]
-        start(i, 3)
+        start(i, 3, 10)
         arrive(i, 1)
         part[i, :, 3, A_DN] += rq2[i]
-        start(i, 4)
+        start(i, 4, 11)
 
     def second(i):
         arrive(i, 3, 4)
-        part[i, :, 0, A_ALL] += fa1[i] + fa3[i]
+        part[i, 1, 0, A_ALL] += fa1[1, i] + fa3[1, i]
         start(i, 7)
 
     def cross(i):
@@ -210,8 +215,8 @@
         start(i, 9)
 
     def finish(i):
-        arrive(i, 7)
-        rows = part[i, 0, 0, A_ALL] + fx2[i]
+        arrive(i, 10, 11, 7)
+        rows = part[i, 0, 0, A_ALL] + (fa1[0, i] + fa3[0, i]) + fx2[i]
         for h in range(2):
             total[2 * i + h, A_ALL] = rows[:, h * WB:(h + 1) * WB]
         arrive(i, 8, 9)
@@ -234,7 +239,8 @@
 
         @pl.when(step == 2)
         def _():
-            pass_on(2, 4)
+            links[4].start()
+            pass_on(2)
             pass_on(3, 5, 6)
             first(1)
 
@@ -242,13 +248,14 @@
         def _():
             first(3)
             pass_on(4)
+            pass_on(6, 7)
+
+        @pl.when(step == 5)
+        def _():
             pass_on(5)
-
-        @pl.when(step == 5)
-        def _():
-            pass_on(6, 7)
-
-        @pl.when(step == 7)
+            first(4)
+
+        @pl.when(step == 6)
         def _():
             pass_on(7)
 
@@ -261,7 +268,7 @@
             links[1].wait_send()
             links[2].start()
 
-        @pl.when((step == 3) | (step >= 5))
+        @pl.when((step == 3) | (step >= 6))
         def _():
             first(step - 1)
 
@@ -294,12 +301,10 @@
 
     for n in range(2, 8):
         links[n].wait_send()
-
-    @pl.loop(0, NCH)
-    def _(i):
-        share(i).wait_send()
-        for copy in reduce_copies(i).values():
-            copy().wait_send()
+    every = slice(None)
+    share(every, 0).wait_send()
+    for copy in reduce_copies(every, 0).values():
+        copy().wait_send()
 
 
 def per_device(lower_inverse, upper_inverse, left_coupling, right_pieces, interface_block, a_gg, panel_order):
@@ -323,13 +328,13 @@
         scratch_shapes=[
             buf(NI, NI), buf(NI, NI), buf(4, WB, NI, dtype=BF16), buf(NCH, 2, NI, WB),
             buf(NI, NI, dtype=BF16), buf(NI, NI, dtype=BF16), buf(NI, NI, dtype=BF16), buf(NI, NI, dtype=BF16),
-            buf(2, 4, WB, NI, dtype=BF16),
+            buf(2, 4 * WB, NI, dtype=BF16),
             buf(NI, CW, dtype=BF16), buf(NI, CW, dtype=BF16), buf(NI, CW, dtype=BF16), buf(NI, CW, dtype=BF16),
             buf(NI, CW, dtype=BF16), buf(NCH, 2, 4, WB, CW),
-            buf(NCH, 2, UP, CW), buf(NCH, 2, DN, CW), buf(NCH, 4, XR, CW), buf(NCH, 2, RA, CW), buf(NCH, 2, RA, CW),
+            buf(NCH, 2, UP, CW), buf(NCH, 2, DN, CW), buf(NCH, 4, XR, CW), buf(2, NCH, RA, CW), buf(2, NCH, RA, CW),
             buf(NCH, XU, CW), buf(NCH, XD, CW), buf(NCH, RA, CW), buf(NCH, XR, CW), buf(NCH, XR, CW),
             buf(WB, a_gg.shape[2]), buf(2 * NCH, WB, WB), pltpu.SMEM((2 * NCH,), jnp.int32),
-            dma((11,)), dma((7,)), dma((NCH,)), dma((NCH,)), dma((NCH,)), dma((NCH, 10)), dma((NCH, 10)),
+            dma((11,)), dma((7,)), dma((NCH,)), dma, dma((NCH,)), dma((12,)), dma((NCH, 12)),
         ],
         compiler_params=pltpu.CompilerParams(
             collective_id=0, has_side_effects=True, vmem_limit_bytes=52 * 2**20),

time: 81.7 us -> 78.3 us (0.958)
  Pallas kernels: 79.9 us -> 76.8 us
    pallas_call x1, Pallas kernels: 79.9 us -> 76.8 us  [per_device(): pl.pallas_call(main_kernel, name='assemble', out_shape=jax.ShapeDtypeStru...]
where the time goes in v3:
time: 78.3 us; the launch traced here: 77.8 us
  Pallas kernels  76.8 us (98%)
  local copies, waits for them, and re-layouts  0.97 us (1%)
    pallas_call x1, Pallas kernels, per_device(): pl.pallas_call(main_kernel, name='assemble', out_shape=jax.ShapeDtypeStru...  76.8 us

profile of v3, /device:TPU:0, one launch (start us, length us, event | category | flops | bytes accessed | tf_op | source)
XLA Modules:
  0.0 77.8 jit_solution(2124386705120258020)
XLA Ops:
  0.0 76.8 %assemble.1 = f32[128,2048]{1,0:T(8,128)S(1)} custom-call(s32[4]{0:T(128)} %bitcast.13, s32[16]{0:T(128)} %order.1, f32[1024,1024]{1,0:T(8,128)} %bitcast.8, f32[1024,1024]{1,0:T(8,128)} %bitcast.9, bf16[4,128,1024]{2,1,0:T(8,128)(2,1)} %bitcast.10, f32[1024,128]{1,0:T(8,128)} %bitcast.12, f32[128,2048]{1,0:T(8,128)} %bitcast.11), custom_call_target="tpu_custom_call" | custom-call | tf_op jit(solution)/shard_map/assemble/pallas_call | solution.py:322
  76.8 1.0 %copy.9 = f32[1,128,2048]{2,1,0:T(8,128)} copy(f32[1,128,2048]{2,1,0:T(8,128)S(1)} %bitcast.7) | data formatting | bytes 2097152

commit v4 on v3

--- a/solution.py
+++ b/solution.py
@@ -25,6 +25,8 @@
 
 CHUNKS = ((0, 0), (-1, 0), (1, 0), (0, 1), (2, 0), (-1, 1), (1, 1), (2, 1))
 
+LEFT_ORDER = tuple((dz, dx) for dz in (2, 1, 3, 0) for dx in (0, 1))
+
 
 def coords():
     r, c = lax.axis_index("row"), lax.axis_index("col")
@@ -44,7 +46,7 @@
     ids, order, low_hbm, upp_hbm, left_hbm, piece_hbm, base_hbm, out,
     low32, upp32, left_v, panel, low_hi, low_lo, upp_hi, upp_lo, left_d,
     p_hi, p_lo, h_hi, h_lo, solved, part,
-    rp2, rq2, rx, fa1, fa3, rxp2, rxq2, fx2, fx1, fx3, base, total, origin,
+    rp2, rq2, rx, up1, dn3, dn1, up3, rxp2, rxq2, fx2, fx1, fx3, base, total, origin,
     loc_sem, ag_s, ag_r, par_s, par_r, rs_s, rs_r,
 ):
     y, xl, core, xh, z = coords()
@@ -117,16 +119,15 @@
             upp_hi[rows, cols], upp_lo[rows, cols] = split(upp32[rows, cols])
 
     left_load.wait()
-    for dx in range(2):
-        for dz in range(4):
-            block = ((xh + dx) % 2) * 4 + (z + dz) % 4
-            place = jnp.int32(0)
-            touched = jnp.int32(0)
-            for k in range(4):
-                hit = ids[k] == block
-                place = jnp.where(hit, k, place)
-                touched = jnp.where(hit, 1, touched)
-            left_d[dx, dz * WB:(dz + 1) * WB] = jnp.where(touched > 0, left_v[place], jnp.zeros((WB, NI), BF16))
+    for n, (dz, dx) in enumerate(LEFT_ORDER):
+        block = ((xh + dx) % 2) * 4 + (z + dz) % 4
+        place = jnp.int32(0)
+        touched = jnp.int32(0)
+        for k in range(4):
+            hit = ids[k] == block
+            place = jnp.where(hit, k, place)
+            touched = jnp.where(hit, 1, touched)
+        left_d[n * WB:(n + 1) * WB] = jnp.where(touched > 0, left_v[place], jnp.zeros((WB, NI), BF16))
 
     def reduce_copies(i, at=None):
         at = i if at is None else at
@@ -141,10 +142,12 @@
             0: lambda: send(0, part.at[i, both, 2, A_UP], rp2, zp),
             1: lambda: send(1, part.at[i, both, 2, A_DN], rq2, zm),
             2: lambda: send(2, part.at[i, 1, both, X_ALL], rx, far),
-            3: lambda: send(3, part.at[i, 1, 1, A_ALL], fa1.at[1], zp),
-            4: lambda: send(4, part.at[i, 1, 3, A_ALL], fa3.at[1], zm),
-            10: lambda: send(10, part.at[i, 0, 1, A_ALL], fa1.at[0], zp),
-            11: lambda: send(11, part.at[i, 0, 3, A_ALL], fa3.at[0], zm),
+            3: lambda: send(3, part.at[i, 1, 1, A_UP], up1.at[1], zp),
+            4: lambda: send(4, part.at[i, 1, 3, A_DN], dn3.at[1], zm),
+            10: lambda: send(10, part.at[i, 0, 1, A_UP], up1.at[0], zp),
+            11: lambda: send(11, part.at[i, 0, 3, A_DN], dn3.at[0], zm),
+            12: lambda: send(12, part.at[i, both, 1, A_DN], dn1, zp),
+            13: lambda: send(13, part.at[i, both, 3, A_UP], up3, zm),
             5: lambda: send(5, part.at[i, 0, 2, X_UP], rxp2, zp),
             6: lambda: send(6, part.at[i, 0, 2, X_DN], rxq2, zm),
             7: lambda: send(7, part.at[i, 1, 0, A_ALL], fx2, far),
@@ -185,8 +188,12 @@
             both = dot(jnp.concatenate([a_hi, upp_lo[rows, cols]], axis=0), h_hi[cols])
             full = both[:TB] + both[TB:] + dot(a_hi, h_lo[cols])
             solved[rows, :] = full.astype(BF16)
-        for dx in range(2):
-            part[i, dx] = dot(left_d[dx], solved[...]).reshape(4, WB, CW)
+        for first_n in (0, 4):
+            blocks = dot(left_d[first_n * WB:(first_n + 4) * WB], solved[...]).reshape(4, WB, CW)
+            for n in range(4):
+                dz, dx = LEFT_ORDER[first_n + n]
+                part[i, dx, dz] = blocks[n]
+        start(i, 0, 1, 12, 13, 2)
 
     def first(i):
         arrive(i, 0)
@@ -197,8 +204,9 @@
         start(i, 4, 11)
 
     def second(i):
-        arrive(i, 3, 4)
-        part[i, 1, 0, A_ALL] += fa1[1, i] + fa3[1, i]
+        arrive(i, 12, 13, 3, 4)
+        part[i, 1, 0, A_UP] += up1[1, i] + up3[i, 1]
+        part[i, 1, 0, A_DN] += dn1[i, 1] + dn3[1, i]
         start(i, 7)
 
     def cross(i):
@@ -216,9 +224,13 @@
 
     def finish(i):
         arrive(i, 10, 11, 7)
-        rows = part[i, 0, 0, A_ALL] + (fa1[0, i] + fa3[0, i]) + fx2[i]
-        for h in range(2):
-            total[2 * i + h, A_ALL] = rows[:, h * WB:(h + 1) * WB]
+        for rows, others in (
+            (A_UP, up1[0, i] + up3[i, 0] + fx2[i, 0:UP]),
+            (A_DN, dn1[i, 0] + dn3[0, i] + fx2[i, UP:RA]),
+        ):
+            summed = part[i, 0, 0, rows] + others
+            for h in range(2):
+                total[2 * i + h, rows] = summed[:, h * WB:(h + 1) * WB]
         arrive(i, 8, 9)
         rows = part[i, 0, 0, X_ALL] + (fx1[i] + fx3[i])
         for h in range(2):
@@ -261,7 +273,6 @@
 
         share(step).wait_recv()
         multiply(step)
-        start(step, 0, 1, 2)
 
         @pl.when(step == 0)
         def _():
@@ -328,13 +339,14 @@
         scratch_shapes=[
             buf(NI, NI), buf(NI, NI), buf(4, WB, NI, dtype=BF16), buf(NCH, 2, NI, WB),
             buf(NI, NI, dtype=BF16), buf(NI, NI, dtype=BF16), buf(NI, NI, dtype=BF16), buf(NI, NI, dtype=BF16),
-            buf(2, 4 * WB, NI, dtype=BF16),
+            buf(8 * WB, NI, dtype=BF16),
             buf(NI, CW, dtype=BF16), buf(NI, CW, dtype=BF16), buf(NI, CW, dtype=BF16), buf(NI, CW, dtype=BF16),
             buf(NI, CW, dtype=BF16), buf(NCH, 2, 4, WB, CW),
-            buf(NCH, 2, UP, CW), buf(NCH, 2, DN, CW), buf(NCH, 4, XR, CW), buf(2, NCH, RA, CW), buf(2, NCH, RA, CW),
+            buf(NCH, 2, UP, CW), buf(NCH, 2, DN, CW), buf(NCH, 4, XR, CW), buf(2, NCH, UP, CW), buf(2, NCH, DN, CW),
+            buf(NCH, 2, DN, CW), buf(NCH, 2, UP, CW),
             buf(NCH, XU, CW), buf(NCH, XD, CW), buf(NCH, RA, CW), buf(NCH, XR, CW), buf(NCH, XR, CW),
             buf(WB, a_gg.shape[2]), buf(2 * NCH, WB, WB), pltpu.SMEM((2 * NCH,), jnp.int32),
-            dma((11,)), dma((7,)), dma((NCH,)), dma, dma((NCH,)), dma((12,)), dma((NCH, 12)),
+            dma((11,)), dma((7,)), dma((NCH,)), dma, dma((NCH,)), dma((14,)), dma((NCH, 14)),
         ],
         compiler_params=pltpu.CompilerParams(
             collective_id=0, has_side_effects=True, vmem_limit_bytes=52 * 2**20),

time: 78.3 us -> 78 us (level)
  no operation moved by 1% of the time
where the time goes in v4:
time: 78 us; the launch traced here: 77.9 us
  Pallas kernels  76.9 us (99%)
  local copies, waits for them, and re-layouts  0.97 us (1%)
    pallas_call x1, Pallas kernels, per_device(): pl.pallas_call(main_kernel, name='assemble', out_shape=jax.ShapeDtypeStru...  76.9 us

profile of v4, /device:TPU:0, one launch (start us, length us, event | category | flops | bytes accessed | tf_op | source)
XLA Modules:
  0.0 77.9 jit_solution(8655285030219084460)
XLA Ops:
  0.0 76.9 %assemble.1 = f32[128,2048]{1,0:T(8,128)S(1)} custom-call(s32[4]{0:T(128)} %bitcast.13, s32[16]{0:T(128)} %order.1, f32[1024,1024]{1,0:T(8,128)} %bitcast.8, f32[1024,1024]{1,0:T(8,128)} %bitcast.9, bf16[4,128,1024]{2,1,0:T(8,128)(2,1)} %bitcast.10, f32[1024,128]{1,0:T(8,128)} %bitcast.12, f32[128,2048]{1,0:T(8,128)} %bitcast.11), custom_call_target="tpu_custom_call" | custom-call | tf_op jit(solution)/shard_map/assemble/pallas_call | solution.py:333
  76.9 1.0 %copy.9 = f32[1,128,2048]{2,1,0:T(8,128)} copy(f32[1,128,2048]{2,1,0:T(8,128)S(1)} %bitcast.7) | data formatting | bytes 2097152

commit v5 on v4

--- a/solution.py
+++ b/solution.py
@@ -27,6 +27,9 @@
 
 LEFT_ORDER = tuple((dz, dx) for dz in (2, 1, 3, 0) for dx in (0, 1))
 
+RING, RINGED = 4, (0, 1, 3, 4, 5, 6)
+LONE = (2, 7, 8, 9, 10, 11, 12, 13)
+
 
 def coords():
     r, c = lax.axis_index("row"), lax.axis_index("col")
@@ -47,7 +50,7 @@
     low32, upp32, left_v, panel, low_hi, low_lo, upp_hi, upp_lo, left_d,
     p_hi, p_lo, h_hi, h_lo, solved, part,
     rp2, rq2, rx, up1, dn3, dn1, up3, rxp2, rxq2, fx2, fx1, fx3, base, total, origin,
-    loc_sem, ag_s, ag_r, par_s, par_r, rs_s, rs_r,
+    loc_sem, ag_s, ag_r, par_s, par_r, rs_s, rs_r, ring_r,
 ):
     y, xl, core, xh, z = coords()
     partner = device(y, xl, 1 - core, xh, z)
@@ -83,7 +86,7 @@
 
     def link(n, src, dst, peer):
         return pltpu.make_async_remote_copy(
-            src_ref=panel.at[src, 0], dst_ref=panel.at[dst, 0], send_sem=ag_s.at[n],
+            src_ref=panel.at[src, 0], dst_ref=panel.at[dst, 0], send_sem=ag_s.at[min(n, 1)],
             recv_sem=ag_r.at[dst], device_id=peer, device_id_type=MESH)
 
     links = {
@@ -100,7 +103,7 @@
     links[1].start()
     links[3].start()
 
-    strip = 32
+    strip = 64
     for b in range(4):
         loads[b].wait()
 
@@ -133,8 +136,9 @@
         at = i if at is None else at
 
         def send(n, src, dst, peer):
+            slot = at % RING if n in RINGED else at
             return pltpu.make_async_remote_copy(
-                src_ref=src, dst_ref=dst.at[i], send_sem=rs_s.at[n], recv_sem=rs_r.at[at, n],
+                src_ref=src, dst_ref=dst.at[i], send_sem=rs_s.at[n], recv_sem=(ring_r if n in RINGED else rs_r).at[slot, (RINGED if n in RINGED else LONE).index(n)],
                 device_id=peer, device_id_type=MESH)
 
         both = slice(None)
@@ -258,8 +262,8 @@
 
         @pl.when(step == 4)
         def _():
+            pass_on(4)
             first(3)
-            pass_on(4)
             pass_on(6, 7)
 
         @pl.when(step == 5)
@@ -310,8 +314,10 @@
         cols = slice(p * WB, (p + 1) * WB)
         out[:, cols] = base[:, cols] - total[origin[p]]
 
-    for n in range(2, 8):
-        links[n].wait_send()
+    six = panel.at[pl.ds(0, 6), 0]
+    others = pltpu.make_async_remote_copy(
+        src_ref=six, dst_ref=six, send_sem=ag_s.at[1], recv_sem=ag_r.at[0], device_id=ahead, device_id_type=MESH)
+    others.wait_send()
     every = slice(None)
     share(every, 0).wait_send()
     for copy in reduce_copies(every, 0).values():
@@ -346,7 +352,7 @@
             buf(NCH, 2, DN, CW), buf(NCH, 2, UP, CW),
             buf(NCH, XU, CW), buf(NCH, XD, CW), buf(NCH, RA, CW), buf(NCH, XR, CW), buf(NCH, XR, CW),
             buf(WB, a_gg.shape[2]), buf(2 * NCH, WB, WB), pltpu.SMEM((2 * NCH,), jnp.int32),
-            dma((11,)), dma((7,)), dma((NCH,)), dma, dma((NCH,)), dma((14,)), dma((NCH, 14)),
+            dma((11,)), dma((2,)), dma((NCH,)), dma, dma((NCH,)), dma((14,)), dma((NCH, len(LONE))), dma((RING, len(RINGED))),
         ],
         compiler_params=pltpu.CompilerParams(
             collective_id=0, has_side_effects=True, vmem_limit_bytes=52 * 2**20),

time: 78 us -> 77.3 us (level)
  no operation moved by 1% of the time
where the time goes in v5:
time: 77.3 us; the launch traced here: 77.2 us
  Pallas kernels  76.2 us (99%)
  local copies, waits for them, and re-layouts  0.97 us (1%)
    pallas_call x1, Pallas kernels, per_device(): pl.pallas_call(main_kernel, name='assemble', out_shape=jax.ShapeDtypeStru...  76.2 us

profile of v5, /device:TPU:0, one launch (start us, length us, event | category | flops | bytes accessed | tf_op | source)
XLA Modules:
  0.0 77.2 jit_solution(10365925117743822046)
XLA Ops:
  0.0 76.2 %assemble.1 = f32[128,2048]{1,0:T(8,128)S(1)} custom-call(s32[4]{0:T(128)} %bitcast.13, s32[16]{0:T(128)} %order.1, f32[1024,1024]{1,0:T(8,128)} %bitcast.8, f32[1024,1024]{1,0:T(8,128)} %bitcast.9, bf16[4,128,1024]{2,1,0:T(8,128)(2,1)} %bitcast.10, f32[1024,128]{1,0:T(8,128)} %bitcast.12, f32[128,2048]{1,0:T(8,128)} %bitcast.11), custom_call_target="tpu_custom_call" | custom-call | tf_op jit(solution)/shard_map/assemble/pallas_call | solution.py:339
  76.2 1.0 %copy.9 = f32[1,128,2048]{2,1,0:T(8,128)} copy(f32[1,128,2048]{2,1,0:T(8,128)S(1)} %bitcast.7) | data formatting | bytes 2097152
